TPU v7x, 32 devices: a whole 2x2x4 slice. The times are simulated.
32 devices in a mesh: groups: 2 (over x), seq: 16 (over z, y, core).
Axes of the slice: x: 2, y: 2, z: 4, core: 2. Of those that a mesh axis runs over, the one named last changes fastest.
Arguments:
- queries: bfloat16 [4096, 1792], P(('groups', 'seq')), parts along dimension 0, may hold values from -100 to 100
- key_rows: bfloat16 [4096, 256], P(('groups', 'seq')), parts along dimension 0, may hold values from -100 to 100
- value_rows: bfloat16 [4096, 256], P(('groups', 'seq')), parts along dimension 0, may hold values from -6 to 6
- span_order: int32 [64], P('groups'), parts along dimension 0, may hold values from 0 to 31, each once
- kept_blocks: int32 [4, 1], P('groups'), parts along dimension 0, may hold values from 0 to 3, as said below
Outputs:
- attended: bfloat16 [4096, 1792], P(('groups', 'seq')), parts along dimension 0
- kept_cache: bfloat16 [1024, 512], P(('groups', 'seq')), parts along dimension 0
There are 2 independent parts, one for each index of `groups`. A program takes and returns all parts, laid end to end along the dimension named above; each array names one. Nothing has to cross between parts.
Inputs may be any that keep to these rules, and one draw needn't show every extreme that they name: `kept_blocks`: each row lists 1 different blocks.
All inputs are finite; a program needn't handle non-finite values.
Results may differ from a plain program's by a relative error of at most 0.0055.
Values may be sent and summed in bfloat16 or wider, within the bound.
A program may use at most 64 MiB of HBM per device.

v0:
```python
import math
import jax
import jax.numpy as jnp
from jax import lax
from jax.sharding import PartitionSpec as P

HEAD_DIM = 128
BLOCK = 512


def token_positions(span_order, span_len):
    within = jnp.arange(span_len, dtype=jnp.int32)
    return (span_order[:, None] * span_len + within[None, :]).reshape(-1)


def cache_sources(kept_blocks, row_ids):
    block_ids = row_ids // BLOCK
    match = (
        jnp.arange(kept_blocks.shape[1], dtype=jnp.int32)[None, None, :] == block_ids[None, :, None]
    )
    chosen = jnp.sum(jnp.where(match, kept_blocks[:, None, :], 0), axis=-1)
    return chosen * BLOCK + row_ids[None, :] % BLOCK


def local(queries, key_rows, value_rows, span_order, kept_blocks):
    seq_count = lax.axis_size("seq")
    my_index = lax.axis_index("seq")
    query_rows = queries.shape[0]
    kv_heads = key_rows.shape[1] // HEAD_DIM
    group_size = queries.shape[1] // key_rows.shape[1]
    scale = 1.0 / math.sqrt(HEAD_DIM)
    positions = token_positions(span_order, query_rows // 2)
    query_pos = lax.dynamic_slice_in_dim(positions, my_index * query_rows, query_rows)
    query_heads = queries.reshape(query_rows, kv_heads, group_size, HEAD_DIM)
    cache_local = kept_blocks.shape[1] * BLOCK // seq_count
    cache_src = cache_sources(
        kept_blocks, my_index * cache_local + jnp.arange(cache_local, dtype=jnp.int32)
    )

    def pick_rows(sources, key_part, value_part, part_pos):
        onehot = (sources[:, :, None] == part_pos[None, None, :]).astype(jnp.bfloat16)
        count = key_part.shape[0]
        out_rows = sources.shape[1]
        picked_keys = jnp.einsum(
            "hrk,khd->rhd",
            onehot,
            key_part.reshape(count, kv_heads, HEAD_DIM),
            preferred_element_type=jnp.float32,
        )
        picked_values = jnp.einsum(
            "hrk,khd->rhd",
            onehot,
            value_part.reshape(count, kv_heads, HEAD_DIM),
            preferred_element_type=jnp.float32,
        )
        return jnp.concatenate(
            [picked_keys.reshape(out_rows, -1), picked_values.reshape(out_rows, -1)], axis=1
        )

    def attend_block(state, block_keys, block_values, block_pos):
        running_max, totals, accum = (state[0], state[1], state[2])
        count = block_keys.shape[0]
        scores = (
            jnp.einsum(
                "qhgd,khd->hgqk",
                query_heads,
                block_keys.reshape(count, kv_heads, HEAD_DIM),
                preferred_element_type=jnp.float32,
            )
            * scale
        )
        visible = block_pos[None, None, None, :] <= query_pos[None, None, :, None]
        scores = jnp.where(visible, scores, -1e30)
        new_max = jnp.maximum(running_max, jnp.max(scores, axis=-1))
        weights = jnp.where(visible, jnp.exp(scores - new_max[..., None]), 0.0)
        factor = jnp.exp(running_max - new_max)
        totals = totals * factor + jnp.sum(weights, axis=-1)
        mixed = jnp.einsum(
            "hgqk,khd->hgqd",
            weights.astype(jnp.bfloat16),
            block_values.reshape(count, kv_heads, HEAD_DIM),
            preferred_element_type=jnp.float32,
        )
        accum = accum * factor[..., None] + mixed
        return (new_max, totals, accum)

    initial = (
        jnp.full((kv_heads, group_size, query_rows), -1e30, jnp.float32),
        jnp.zeros((kv_heads, group_size, query_rows), jnp.float32),
        jnp.zeros((kv_heads, group_size, query_rows, HEAD_DIM), jnp.float32),
    )
    initial = initial + (jnp.zeros((cache_local, 2 * kv_heads * HEAD_DIM), jnp.float32),)
    piece_keys = lax.all_gather(key_rows, "seq", axis=0, tiled=True)
    piece_values = lax.all_gather(value_rows, "seq", axis=0, tiled=True)
    count = piece_keys.shape[0]
    width = math.gcd(count, 512)

    def inner(step_index, inner_state):
        offset = (step_index * width).astype(jnp.int32)
        block_keys = lax.dynamic_slice_in_dim(piece_keys, offset, width, 0)
        block_values = lax.dynamic_slice_in_dim(piece_values, offset, width, 0)
        block_pos = lax.dynamic_slice_in_dim(positions, offset, width)
        updated = attend_block(inner_state, block_keys, block_values, block_pos)
        extra = (inner_state[3] + pick_rows(cache_src, block_keys, block_values, block_pos),)
        return updated + extra

    final = lax.fori_loop(0, count // width, inner, initial)
    attended = final[2] / final[1][..., None]
    attended = jnp.transpose(attended, (2, 0, 1, 3)).reshape(query_rows, -1).astype(jnp.bfloat16)
    kept_cache = final[3].astype(jnp.bfloat16)
    return (attended, kept_cache)


def solution(mesh):
    placed = (
        P(("groups", "seq"), None),
        P(("groups", "seq"), None),
        P(("groups", "seq"), None),
        P("groups"),
        P("groups", None),
    )
    return jax.shard_map(
        local,
        mesh=mesh,
        in_specs=placed,
        out_specs=(P(("groups", "seq"), None), P(("groups", "seq"), None)),
        check_vma=False,
    )
```

profile of v0, /device:TPU:0, one launch (start us, length us, event | category | flops | bytes accessed | tf_op | source)
XLA Modules:
  0.0 120.7 jit_solution(2158012903326060525)
XLA Ops:
  7.2 1.6 %copy.16 = bf16[128,256]{0,1:T(8,128)(2,1)} copy(bf16[128,256]{1,0:T(8,128)(2,1)} %param.8) | data formatting | bytes 131072 | tf_op args[1]
  8.9 1.6 %copy.18 = bf16[128,256]{0,1:T(8,128)(2,1)} copy(bf16[128,256]{1,0:T(8,128)(2,1)} %param.9) | data formatting | bytes 131072 | tf_op args[2]
  10.5 0.7 broadcast_multiply_fusion
  11.3 1.3 %copy.17 = bf16[128,1792]{0,1:T(8,128)(2,1)S(1)} copy(bf16[128,1792]{1,0:T(8,128)(2,1)} %param.7) | data formatting | bytes 917504 | tf_op args[0]
  12.6 0.3 copy.19
  12.9 0.1 dynamic_slice.24
  13.0 37.1 %all-gather.3.cloned.1.call-done = bf16[2048,256]{0,1:T(8,128)(2,1)} async-done(((bf16[128,256]{0,1:T(8,128)(2,1)}), bf16[2048,256]{0,1:T(8,128)(2,1)}) %all-gather.3.cloned.1.call-update) | async-done | bytes 1048592 | tf_op jit(solution)/shard_map/all_gather | solution.py:93
  50.1 38.4 %all-gather.5.cloned.1.call-done = bf16[2048,256]{0,1:T(8,128)(2,1)} async-done(((bf16[128,256]{0,1:T(8,128)(2,1)}), bf16[2048,256]{0,1:T(8,128)(2,1)}) %all-gather.5.cloned.1.call-update) | async-done | bytes 1048592 | tf_op jit(solution)/shard_map/all_gather | solution.py:94
  88.5 23.3 %while.20 = (s32[]{:T(128)}, f32[2,7,128]{2,1,0:T(8,128)S(1)}, f32[2,7,128]{2,1,0:T(8,128)S(1)}, f32[2,7,128,128]{3,2,1,0:T(8,128)S(1)}, f32[32,512]{1,0:T(8,128...) while((s32[]{:T(128)}, f32[2,7,128]{2,1,0:T(8,128)S(1)}, ...), condition=%wide.region_3.4_spmd.clone, body=%wide.region_0.3_spmd.clone.sunk | while | flops 499344320 | bytes 16182928 | solution.py:107
  88.5 0.7 multiply_add_fusion.2
  89.3 0.1 dynamic_slice.33
  89.3 0.1 broadcast_compare_fusion.2
  89.5 1.1 constant_dynamic-slice_fusion.3
  90.6 0.2 convolution_bitcast_fusion.4
  90.8 0.2 convolution_bitcast_fusion.5
  91.1 0.8 fusion.47
  91.9 0.9 fusion.48
  92.8 1.5 %fusion.50 = f32[2,7,128,128]{3,2,1,0:T(8,128)S(1)} fusion(bf16[512,2,128,1]{0,2,3,1:T(8,128)(2,1)S(1)} %bitcast.80, f32[2,512,128,7]{2,1,3,0:T(8,128)S(1)} %get-tuple-element.372, f32[2,7,128]{2,1,0:T(8,128)S(1)} %select_maximum_fusion.2, pred[128,512]{0,1:T(8,128)(4,1)S(1)} %broadcast_compare_fusion.2, ...), kind=kOutput, calls=%fused_computation.8.clone.1 | convolution fusion | flops 240156672 | bytes 5847041 | tf_op jit(solution)/shard_map/while/body/eval_jaxpr/hgqk,khd->hgqd/dot_general | solution.py:78
  94.4 0.7 multiply_add_fusion.2
  95.1 0.1 dynamic_slice.33
  95.2 0.1 broadcast_compare_fusion.2
  95.3 1.1 constant_dynamic-slice_fusion.3
  96.4 0.2 convolution_bitcast_fusion.4
  96.6 0.2 convolution_bitcast_fusion.5
  96.9 0.8 fusion.47
  97.7 0.9 fusion.48
  98.6 1.5 %fusion.50 = f32[2,7,128,128]{3,2,1,0:T(8,128)S(1)} fusion(bf16[512,2,128,1]{0,2,3,1:T(8,128)(2,1)S(1)} %bitcast.80, f32[2,512,128,7]{2,1,3,0:T(8,128)S(1)} %get-tuple-element.372, f32[2,7,128]{2,1,0:T(8,128)S(1)} %select_maximum_fusion.2, pred[128,512]{0,1:T(8,128)(4,1)S(1)} %broadcast_compare_fusion.2, ...), kind=kOutput, calls=%fused_computation.8.clone.1 | convolution fusion | flops 240156672 | bytes 5847041 | tf_op jit(solution)/shard_map/while/body/eval_jaxpr/hgqk,khd->hgqd/dot_general | solution.py:78
  100.2 0.7 multiply_add_fusion.2
  100.9 0.1 dynamic_slice.33
  101.0 0.1 broadcast_compare_fusion.2
  101.1 1.1 constant_dynamic-slice_fusion.3
  102.2 0.2 convolution_bitcast_fusion.4
  102.4 0.2 convolution_bitcast_fusion.5
  102.7 0.8 fusion.47
  103.5 0.9 fusion.48
  104.4 1.5 %fusion.50 = f32[2,7,128,128]{3,2,1,0:T(8,128)S(1)} fusion(bf16[512,2,128,1]{0,2,3,1:T(8,128)(2,1)S(1)} %bitcast.80, f32[2,512,128,7]{2,1,3,0:T(8,128)S(1)} %get-tuple-element.372, f32[2,7,128]{2,1,0:T(8,128)S(1)} %select_maximum_fusion.2, pred[128,512]{0,1:T(8,128)(4,1)S(1)} %broadcast_compare_fusion.2, ...), kind=kOutput, calls=%fused_computation.8.clone.1 | convolution fusion | flops 240156672 | bytes 5847041 | tf_op jit(solution)/shard_map/while/body/eval_jaxpr/hgqk,khd->hgqd/dot_general | solution.py:78
  106.0 0.7 multiply_add_fusion.2
  106.8 0.1 broadcast_compare_fusion.2
  106.9 1.1 constant_dynamic-slice_fusion.3
  108.0 0.2 convolution_bitcast_fusion.4
  108.3 0.2 convolution_bitcast_fusion.5
  108.5 0.8 fusion.47
  109.3 0.9 fusion.48
  110.2 1.5 %fusion.50 = f32[2,7,128,128]{3,2,1,0:T(8,128)S(1)} fusion(bf16[512,2,128,1]{0,2,3,1:T(8,128)(2,1)S(1)} %bitcast.80, f32[2,512,128,7]{2,1,3,0:T(8,128)S(1)} %get-tuple-element.372, f32[2,7,128]{2,1,0:T(8,128)S(1)} %select_maximum_fusion.2, pred[128,512]{0,1:T(8,128)(4,1)S(1)} %broadcast_compare_fusion.2, ...), kind=kOutput, calls=%fused_computation.8.clone.1 | convolution fusion | flops 240156672 | bytes 5847041 | tf_op jit(solution)/shard_map/while/body/eval_jaxpr/hgqk,khd->hgqd/dot_general | solution.py:78
  111.8 0.3 copy.20
  112.1 0.1 divide_convert_fusion
  112.2 1.0 copy.21
  113.2 0.6 convert_element_type.25
  (37 shorter events, 0.6 us)
Async XLA Ops:
  7.2 42.9 %all-gather.3.cloned.1.call-start = ((), (), s32[]{:S(2)}) async-start(), calls=%async_computation | async-start | bytes 1114112 | tf_op jit(solution)/shard_map/all_gather | solution.py:93
  8.8 79.7 %all-gather.5.cloned.1.call-start = ((), (), s32[]{:S(2)}) async-start(), calls=%async_computation.1 | async-start | bytes 1114112 | tf_op jit(solution)/shard_map/all_gather | solution.py:94
Sparse Core Ops, SparseCore 0:
  10.7 39.3 all-gather.2
  52.3 36.2 all-gather.4
where the time goes:
time: 121 us
  waiting for transfers between devices  75.6 us (62%)
  between operations  14.1 us (12%)
  matrix products  11 us (9%)
  local copies, waits for them, and re-layouts  10.8 us (9%)
  other arithmetic  8.65 us (7%)
    all_gather x1, waiting for transfers between devices, local(): piece_values = lax.all_gather(value_rows, 'seq', axis=0, tiled=True)  38.4 us
    all_gather x1, waiting for transfers between devices, local(): piece_keys = lax.all_gather(key_rows, 'seq', axis=0, tiled=True)  37.1 us
    dot_general x4, matrix products, attend_block(): jnp.einsum('hgqk,khd->hgqd', weights.astype(jnp.bfloat16), block_values.r...  6.16 us
    unnamed x5, local copies, waits for them, and re-layouts  5.68 us
    dynamic_slice x4, local copies, waits for them, and re-layouts, inner(): block_values = lax.dynamic_slice_in_dim(piece_values, offset, width, 0)  4.29 us
    reduce_sum x4, other arithmetic, attend_block(): totals = totals * factor + jnp.sum(weights, axis=-1)  3.54 us
    dot_general x4, matrix products, attend_block(): jnp.einsum('qhgd,khd->hgqk', query_heads, block_keys.reshape(count, kv_he...  3.13 us
    add x4, other arithmetic, cache_sources(): return chosen * BLOCK + row_ids[None, :] % BLOCK  2.91 us
  transfers between devices with their start and end apart: 2, of which 2 were waited for; matrix products, arithmetic and copies ran while one was open for 3% of the time, Pallas kernels for 0%

commit v1 on v0

--- a/solution.py
+++ b/solution.py
@@ -91,7 +91,12 @@
     )
     initial = initial + (jnp.zeros((cache_local, 2 * kv_heads * HEAD_DIM), jnp.float32),)
     piece_keys = lax.all_gather(key_rows, "seq", axis=0, tiled=True)
-    piece_values = lax.all_gather(value_rows, "seq", axis=0, tiled=True)
+    ring = [value_rows]
+    for hop in range(15):
+        ring.append(lax.ppermute(ring[-1], "seq", [(dev, (dev + 1) % 16) for dev in range(16)]))
+    piece_values = jnp.roll(
+        jnp.concatenate(ring[::-1], axis=0), (lax.axis_index("seq") + 1) * ring[0].shape[0], axis=0
+    )
     count = piece_keys.shape[0]
     width = math.gcd(count, 512)
 

time: 121 us -> 143 us (1.18)
  waiting for transfers between devices: 75.6 us -> 99.8 us
  other arithmetic: 8.65 us -> 6.02 us
    ppermute x0 -> x15, waiting for transfers between devices: none -> 92.5 us  [local(): lax.ppermute(ring[-1], 'seq', [(dev, (dev + 1) % 16) for dev in range(16)])]
    all_gather x1 -> x0, waiting for transfers between devices: 38.4 us -> none  [local(): piece_values = lax.all_gather(value_rows, 'seq', axis=0, tiled=True)]
    all_gather x1, waiting for transfers between devices: 37.1 us -> 7.25 us  [local(): piece_keys = lax.all_gather(key_rows, 'seq', axis=0, tiled=True)]
    add x4, other arithmetic: 2.91 us -> 0.29 us  [cache_sources(): return chosen * BLOCK + row_ids[None, :] % BLOCK]
    unnamed x5 -> x38, local copies, waits for them, and re-layouts: 5.68 us -> 5.66 us
  transfers between devices with their start and end apart: 2 -> 16, of which waited for: 2 -> 16; matrix products, arithmetic and copies ran while one was open for 3% -> 3% of each run, Pallas kernels for 0% -> 0%
where the time goes in v1:
time: 143 us
  waiting for transfers between devices  99.8 us (70%)
  between operations  14.3 us (10%)
  matrix products  11 us (8%)
  local copies, waits for them, and re-layouts  10.6 us (7%)
  other arithmetic  6.02 us (4%)
    ppermute x15, waiting for transfers between devices, local(): lax.ppermute(ring[-1], 'seq', [(dev, (dev + 1) % 16) for dev in range(16)])  92.5 us
    all_gather x1, waiting for transfers between devices, local(): piece_keys = lax.all_gather(key_rows, 'seq', axis=0, tiled=True)  7.25 us
    dot_general x4, matrix products, attend_block(): jnp.einsum('hgqk,khd->hgqd', weights.astype(jnp.bfloat16), block_values.r...  6.16 us
    unnamed x38, local copies, waits for them, and re-layouts  5.66 us
    dynamic_slice x4, local copies, waits for them, and re-layouts, inner(): block_values = lax.dynamic_slice_in_dim(piece_values, offset, width, 0)  4 us
    reduce_sum x4, other arithmetic, attend_block(): totals = totals * factor + jnp.sum(weights, axis=-1)  3.54 us
    dot_general x4, matrix products, attend_block(): jnp.einsum('qhgd,khd->hgqk', query_heads, block_keys.reshape(count, kv_he...  3.13 us
  transfers between devices with their start and end apart: 16, of which 16 were waited for; matrix products, arithmetic and copies ran while one was open for 3% of the time, Pallas kernels for 0%

profile of v1, /device:TPU:0, one launch (start us, length us, event | category | flops | bytes accessed | tf_op | source)
XLA Modules:
  0.0 142.8 jit_solution(8859586658509027111)
XLA Ops:
  7.2 0.9 copy.18
  8.2 0.5 collective-permute-start
  8.7 6.9 %collective-permute-done = bf16[128,256]{0,1:T(8,128)(2,1)S(1)} collective-permute-done((bf16[128,256]{0,1:T(8,128)(2,1)S(1)}, bf16[128,256]{0,1:T(8,128)(2,1)S(1)}, u32[]{:S(2)}, u32[]{:S(2)}) %collective-permute-start) | collective-permute-done | bytes 65568 | tf_op jit(solution)/shard_map/ppermute | solution.py:96
  15.6 6.4 %collective-permute-done.1 = bf16[128,256]{0,1:T(8,128)(2,1)S(1)} collective-permute-done((bf16[128,256]{0,1:T(8,128)(2,1)S(1)}, bf16[128,256]{0,1:T(8,128)(2,1)S(1)}, u32[]{:S(2)}, u32[]{:S(2)}) %collective-permute-start.1) | collective-permute-done | bytes 65568 | tf_op jit(solution)/shard_map/ppermute | solution.py:96
  22.0 6.4 %collective-permute-done.2 = bf16[128,256]{0,1:T(8,128)(2,1)S(1)} collective-permute-done((bf16[128,256]{0,1:T(8,128)(2,1)S(1)}, bf16[128,256]{0,1:T(8,128)(2,1)S(1)}, u32[]{:S(2)}, u32[]{:S(2)}) %collective-permute-start.2) | collective-permute-done | bytes 65568 | tf_op jit(solution)/shard_map/ppermute | solution.py:96
  28.4 6.4 %collective-permute-done.3 = bf16[128,256]{0,1:T(8,128)(2,1)S(1)} collective-permute-done((bf16[128,256]{0,1:T(8,128)(2,1)S(1)}, bf16[128,256]{0,1:T(8,128)(2,1)S(1)}, u32[]{:S(2)}, u32[]{:S(2)}) %collective-permute-start.3) | collective-permute-done | bytes 65568 | tf_op jit(solution)/shard_map/ppermute | solution.py:96
  34.8 6.4 %collective-permute-done.4 = bf16[128,256]{0,1:T(8,128)(2,1)S(1)} collective-permute-done((bf16[128,256]{0,1:T(8,128)(2,1)S(1)}, bf16[128,256]{0,1:T(8,128)(2,1)S(1)}, u32[]{:S(2)}, u32[]{:S(2)}) %collective-permute-start.4) | collective-permute-done | bytes 65568 | tf_op jit(solution)/shard_map/ppermute | solution.py:96
  41.2 6.4 %collective-permute-done.5 = bf16[128,256]{0,1:T(8,128)(2,1)S(1)} collective-permute-done((bf16[128,256]{0,1:T(8,128)(2,1)S(1)}, bf16[128,256]{0,1:T(8,128)(2,1)S(1)}, u32[]{:S(2)}, u32[]{:S(2)}) %collective-permute-start.5) | collective-permute-done | bytes 65568 | tf_op jit(solution)/shard_map/ppermute | solution.py:96
  47.6 6.4 %collective-permute-done.6 = bf16[128,256]{0,1:T(8,128)(2,1)S(1)} collective-permute-done((bf16[128,256]{0,1:T(8,128)(2,1)S(1)}, bf16[128,256]{0,1:T(8,128)(2,1)S(1)}, u32[]{:S(2)}, u32[]{:S(2)}) %collective-permute-start.6) | collective-permute-done | bytes 65568 | tf_op jit(solution)/shard_map/ppermute | solution.py:96
  54.0 6.4 %collective-permute-done.7 = bf16[128,256]{0,1:T(8,128)(2,1)S(1)} collective-permute-done((bf16[128,256]{0,1:T(8,128)(2,1)S(1)}, bf16[128,256]{0,1:T(8,128)(2,1)S(1)}, u32[]{:S(2)}, u32[]{:S(2)}) %collective-permute-start.7) | collective-permute-done | bytes 65568 | tf_op jit(solution)/shard_map/ppermute | solution.py:96
  60.4 6.4 %collective-permute-done.8 = bf16[128,256]{0,1:T(8,128)(2,1)S(1)} collective-permute-done((bf16[128,256]{0,1:T(8,128)(2,1)S(1)}, bf16[128,256]{0,1:T(8,128)(2,1)S(1)}, u32[]{:S(2)}, u32[]{:S(2)}) %collective-permute-start.8) | collective-permute-done | bytes 65568 | tf_op jit(solution)/shard_map/ppermute | solution.py:96
  66.8 6.4 %collective-permute-done.9 = bf16[128,256]{0,1:T(8,128)(2,1)S(1)} collective-permute-done((bf16[128,256]{0,1:T(8,128)(2,1)S(1)}, bf16[128,256]{0,1:T(8,128)(2,1)S(1)}, u32[]{:S(2)}, u32[]{:S(2)}) %collective-permute-start.9) | collective-permute-done | bytes 65568 | tf_op jit(solution)/shard_map/ppermute | solution.py:96
  73.1 1.6 %copy.16 = bf16[128,256]{0,1:T(8,128)(2,1)} copy(bf16[128,256]{1,0:T(8,128)(2,1)} %param.8) | data formatting | bytes 131072 | tf_op args[1]
  74.7 4.8 %collective-permute-done.10 = bf16[128,256]{0,1:T(8,128)(2,1)S(1)} collective-permute-done((bf16[128,256]{0,1:T(8,128)(2,1)S(1)}, bf16[128,256]{0,1:T(8,128)(2,1)S(1)}, u32[]{:S(2)}, u32[]{:S(2)}) %collective-permute-start.10) | collective-permute-done | bytes 65568 | tf_op jit(solution)/shard_map/ppermute | solution.py:96
  79.5 0.7 broadcast_multiply_fusion
  80.2 5.7 %collective-permute-done.11 = bf16[128,256]{0,1:T(8,128)(2,1)S(1)} collective-permute-done((bf16[128,256]{0,1:T(8,128)(2,1)S(1)}, bf16[128,256]{0,1:T(8,128)(2,1)S(1)}, u32[]{:S(2)}, u32[]{:S(2)}) %collective-permute-start.11) | collective-permute-done | bytes 65568 | tf_op jit(solution)/shard_map/ppermute | solution.py:96
  86.1 1.3 copy.17
  87.3 0.3 copy.21
  87.7 4.8 %collective-permute-done.12 = bf16[128,256]{0,1:T(8,128)(2,1)S(1)} collective-permute-done((bf16[128,256]{0,1:T(8,128)(2,1)S(1)}, bf16[128,256]{0,1:T(8,128)(2,1)S(1)}, u32[]{:S(2)}, u32[]{:S(2)}) %collective-permute-start.12) | collective-permute-done | bytes 65568 | tf_op jit(solution)/shard_map/ppermute | solution.py:96
  92.5 6.4 %collective-permute-done.13 = bf16[128,256]{0,1:T(8,128)(2,1)S(1)} collective-permute-done((bf16[128,256]{0,1:T(8,128)(2,1)S(1)}, bf16[128,256]{0,1:T(8,128)(2,1)S(1)}, u32[]{:S(2)}, u32[]{:S(2)}) %collective-permute-start.13) | collective-permute-done | bytes 65568 | tf_op jit(solution)/shard_map/ppermute | solution.py:96
  98.9 6.5 %collective-permute-done.14 = bf16[128,256]{0,1:T(8,128)(2,1)S(1)} collective-permute-done((bf16[128,256]{0,1:T(8,128)(2,1)S(1)}, bf16[128,256]{0,1:T(8,128)(2,1)S(1)}, u32[]{:S(2)}, u32[]{:S(2)}) %collective-permute-start.14) | collective-permute-done | bytes 65568 | tf_op jit(solution)/shard_map/ppermute | solution.py:96
  106.3 7.2 %all-gather.2.cloned.1.call-done = bf16[2048,256]{0,1:T(8,128)(2,1)} async-done(((bf16[128,256]{0,1:T(8,128)(2,1)}), bf16[2048,256]{0,1:T(8,128)(2,1)}) %all-gather.2.cloned.1.call-update) | async-done | bytes 1048592 | tf_op jit(solution)/shard_map/all_gather | solution.py:93
  113.5 20.4 %while.20 = (s32[]{:T(128)}, f32[2,7,128]{2,1,0:T(8,128)S(1)}, f32[2,7,128]{2,1,0:T(8,128)S(1)}, f32[2,7,128,128]{3,2,1,0:T(8,128)S(1)}, f32[32,512]{1,0:T(8,128...) while((s32[]{:T(128)}, f32[2,7,128]{2,1,0:T(8,128)S(1)}, ...), condition=%wide.region_3.4_spmd.clone, body=%wide.region_0.3_spmd.clone.sunk | while | flops 499344320 | bytes 16182928 | solution.py:112
  113.8 1.0 constant_dynamic-slice_fusion.4
  114.8 0.2 convolution_bitcast_fusion.4
  115.1 0.2 convolution_bitcast_fusion.5
  115.3 0.8 fusion.47
  116.1 0.9 fusion.48
  117.1 1.5 %fusion.50 = f32[2,7,128,128]{3,2,1,0:T(8,128)S(1)} fusion(bf16[512,2,128,1]{0,2,3,1:T(8,128)(2,1)S(1)} %bitcast.80, f32[2,512,128,7]{2,1,3,0:T(8,128)S(1)} %get-tuple-element.372, f32[2,7,128]{2,1,0:T(8,128)S(1)} %select_maximum_fusion.2, pred[128,512]{0,1:T(8,128)(4,1)S(1)} %broadcast_compare_fusion.2, ...), kind=kOutput, calls=%fused_computation.8.clone.1 | convolution fusion | flops 240156672 | bytes 5847041 | tf_op jit(solution)/shard_map/while/body/eval_jaxpr/hgqk,khd->hgqd/dot_general | solution.py:78
  118.9 1.0 constant_dynamic-slice_fusion.4
  120.2 0.2 convolution_bitcast_fusion.5
  120.4 0.8 fusion.47
  121.2 0.9 fusion.48
  122.1 1.5 %fusion.50 = f32[2,7,128,128]{3,2,1,0:T(8,128)S(1)} fusion(bf16[512,2,128,1]{0,2,3,1:T(8,128)(2,1)S(1)} %bitcast.80, f32[2,512,128,7]{2,1,3,0:T(8,128)S(1)} %get-tuple-element.372, f32[2,7,128]{2,1,0:T(8,128)S(1)} %select_maximum_fusion.2, pred[128,512]{0,1:T(8,128)(4,1)S(1)} %broadcast_compare_fusion.2, ...), kind=kOutput, calls=%fused_computation.8.clone.1 | convolution fusion | flops 240156672 | bytes 5847041 | tf_op jit(solution)/shard_map/while/body/eval_jaxpr/hgqk,khd->hgqd/dot_general | solution.py:78
  124.0 1.0 constant_dynamic-slice_fusion.4
  125.0 0.2 convolution_bitcast_fusion.4
  125.3 0.2 convolution_bitcast_fusion.5
  125.5 0.8 fusion.47
  126.3 0.9 fusion.48
  127.2 1.5 %fusion.50 = f32[2,7,128,128]{3,2,1,0:T(8,128)S(1)} fusion(bf16[512,2,128,1]{0,2,3,1:T(8,128)(2,1)S(1)} %bitcast.80, f32[2,512,128,7]{2,1,3,0:T(8,128)S(1)} %get-tuple-element.372, f32[2,7,128]{2,1,0:T(8,128)S(1)} %select_maximum_fusion.2, pred[128,512]{0,1:T(8,128)(4,1)S(1)} %broadcast_compare_fusion.2, ...), kind=kOutput, calls=%fused_computation.8.clone.1 | convolution fusion | flops 240156672 | bytes 5847041 | tf_op jit(solution)/shard_map/while/body/eval_jaxpr/hgqk,khd->hgqd/dot_general | solution.py:78
  129.1 1.0 constant_dynamic-slice_fusion.4
  130.4 0.2 convolution_bitcast_fusion.5
  130.6 0.8 fusion.47
  131.4 0.9 fusion.48
  132.3 1.5 %fusion.50 = f32[2,7,128,128]{3,2,1,0:T(8,128)S(1)} fusion(bf16[512,2,128,1]{0,2,3,1:T(8,128)(2,1)S(1)} %bitcast.80, f32[2,512,128,7]{2,1,3,0:T(8,128)S(1)} %get-tuple-element.372, f32[2,7,128]{2,1,0:T(8,128)S(1)} %select_maximum_fusion.2, pred[128,512]{0,1:T(8,128)(4,1)S(1)} %broadcast_compare_fusion.2, ...), kind=kOutput, calls=%fused_computation.8.clone.1 | convolution fusion | flops 240156672 | bytes 5847041 | tf_op jit(solution)/shard_map/while/body/eval_jaxpr/hgqk,khd->hgqd/dot_general | solution.py:78
  133.9 0.3 copy.22
  134.3 1.0 copy.23
  135.3 0.6 convert_element_type.25
  (99 shorter events, 3.0 us)
Async XLA Ops:
  7.2 106.4 %all-gather.2.cloned.1.call-start = ((), (), s32[]{:S(2)}) async-start(), calls=%async_computation | async-start | bytes 1114112 | tf_op jit(solution)/shard_map/all_gather | solution.py:93
  8.2 7.5 %collective-permute-start = (bf16[128,256]{0,1:T(8,128)(2,1)S(1)}, bf16[128,256]{0,1:T(8,128)(2,1)S(1)}, u32[]{:S(2)}, u32[]{:S(2)}) collective-permute-start(bf16[128,256]{0,1:T(8,128)(2,1)S(1)} %copy.18), channel_id=1, source_target_pairs={{0,1},{1,2},{2,3},{3,4},{4,5},{5,6},{6,7},{7,8},{8,9},{9,10},{10,1... | collective-permute-start | bytes 196616 | tf_op jit(solution)/shard_map/ppermute | solution.py:96
  15.6 6.4 %collective-permute-start.1 = (bf16[128,256]{0,1:T(8,128)(2,1)S(1)}, bf16[128,256]{0,1:T(8,128)(2,1)S(1)}, u32[]{:S(2)}, u32[]{:S(2)}) collective-permute-start(bf16[128,256]{0,1:T(8,128)(2,1)S(1)} %collective-permute-done), channel_id=1, source_target_pairs={{0,1},{1,2},{2,3},{3,4},{4,5},{5,6},{6,7},{7,8},{8,9},{9,10},{10,1... | collective-permute-start | bytes 196616 | tf_op jit(solution)/shard_map/ppermute | solution.py:96
  22.0 6.4 %collective-permute-start.2 = (bf16[128,256]{0,1:T(8,128)(2,1)S(1)}, bf16[128,256]{0,1:T(8,128)(2,1)S(1)}, u32[]{:S(2)}, u32[]{:S(2)}) collective-permute-start(bf16[128,256]{0,1:T(8,128)(2,1)S(1)} %collective-permute-done.1), channel_id=1, source_target_pairs={{0,1},{1,2},{2,3},{3,4},{4,5},{5,6},{6,7},{7,8},{8,9},{9,10},{10,1... | collective-permute-start | bytes 196616 | tf_op jit(solution)/shard_map/ppermute | solution.py:96
  28.4 6.4 %collective-permute-start.3 = (bf16[128,256]{0,1:T(8,128)(2,1)S(1)}, bf16[128,256]{0,1:T(8,128)(2,1)S(1)}, u32[]{:S(2)}, u32[]{:S(2)}) collective-permute-start(bf16[128,256]{0,1:T(8,128)(2,1)S(1)} %collective-permute-done.2), channel_id=1, source_target_pairs={{0,1},{1,2},{2,3},{3,4},{4,5},{5,6},{6,7},{7,8},{8,9},{9,10},{10,1... | collective-permute-start | bytes 196616 | tf_op jit(solution)/shard_map/ppermute | solution.py:96
  34.8 6.4 %collective-permute-start.4 = (bf16[128,256]{0,1:T(8,128)(2,1)S(1)}, bf16[128,256]{0,1:T(8,128)(2,1)S(1)}, u32[]{:S(2)}, u32[]{:S(2)}) collective-permute-start(bf16[128,256]{0,1:T(8,128)(2,1)S(1)} %collective-permute-done.3), channel_id=1, source_target_pairs={{0,1},{1,2},{2,3},{3,4},{4,5},{5,6},{6,7},{7,8},{8,9},{9,10},{10,1... | collective-permute-start | bytes 196616 | tf_op jit(solution)/shard_map/ppermute | solution.py:96
  41.2 6.4 %collective-permute-start.5 = (bf16[128,256]{0,1:T(8,128)(2,1)S(1)}, bf16[128,256]{0,1:T(8,128)(2,1)S(1)}, u32[]{:S(2)}, u32[]{:S(2)}) collective-permute-start(bf16[128,256]{0,1:T(8,128)(2,1)S(1)} %collective-permute-done.4), channel_id=1, source_target_pairs={{0,1},{1,2},{2,3},{3,4},{4,5},{5,6},{6,7},{7,8},{8,9},{9,10},{10,1... | collective-permute-start | bytes 196616 | tf_op jit(solution)/shard_map/ppermute | solution.py:96
  47.6 6.4 %collective-permute-start.6 = (bf16[128,256]{0,1:T(8,128)(2,1)S(1)}, bf16[128,256]{0,1:T(8,128)(2,1)S(1)}, u32[]{:S(2)}, u32[]{:S(2)}) collective-permute-start(bf16[128,256]{0,1:T(8,128)(2,1)S(1)} %collective-permute-done.5), channel_id=1, source_target_pairs={{0,1},{1,2},{2,3},{3,4},{4,5},{5,6},{6,7},{7,8},{8,9},{9,10},{10,1... | collective-permute-start | bytes 196616 | tf_op jit(solution)/shard_map/ppermute | solution.py:96
  54.0 6.4 %collective-permute-start.7 = (bf16[128,256]{0,1:T(8,128)(2,1)S(1)}, bf16[128,256]{0,1:T(8,128)(2,1)S(1)}, u32[]{:S(2)}, u32[]{:S(2)}) collective-permute-start(bf16[128,256]{0,1:T(8,128)(2,1)S(1)} %collective-permute-done.6), channel_id=1, source_target_pairs={{0,1},{1,2},{2,3},{3,4},{4,5},{5,6},{6,7},{7,8},{8,9},{9,10},{10,1... | collective-permute-start | bytes 196616 | tf_op jit(solution)/shard_map/ppermute | solution.py:96
  60.4 6.4 %collective-permute-start.8 = (bf16[128,256]{0,1:T(8,128)(2,1)S(1)}, bf16[128,256]{0,1:T(8,128)(2,1)S(1)}, u32[]{:S(2)}, u32[]{:S(2)}) collective-permute-start(bf16[128,256]{0,1:T(8,128)(2,1)S(1)} %collective-permute-done.7), channel_id=1, source_target_pairs={{0,1},{1,2},{2,3},{3,4},{4,5},{5,6},{6,7},{7,8},{8,9},{9,10},{10,1... | collective-permute-start | bytes 196616 | tf_op jit(solution)/shard_map/ppermute | solution.py:96
  66.7 6.4 %collective-permute-start.9 = (bf16[128,256]{0,1:T(8,128)(2,1)S(1)}, bf16[128,256]{0,1:T(8,128)(2,1)S(1)}, u32[]{:S(2)}, u32[]{:S(2)}) collective-permute-start(bf16[128,256]{0,1:T(8,128)(2,1)S(1)} %collective-permute-done.8), channel_id=1, source_target_pairs={{0,1},{1,2},{2,3},{3,4},{4,5},{5,6},{6,7},{7,8},{8,9},{9,10},{10,1... | collective-permute-start | bytes 196616 | tf_op jit(solution)/shard_map/ppermute | solution.py:96
  73.1 6.4 %collective-permute-start.10 = (bf16[128,256]{0,1:T(8,128)(2,1)S(1)}, bf16[128,256]{0,1:T(8,128)(2,1)S(1)}, u32[]{:S(2)}, u32[]{:S(2)}) collective-permute-start(bf16[128,256]{0,1:T(8,128)(2,1)S(1)} %collective-permute-done.9), channel_id=1, source_target_pairs={{0,1},{1,2},{2,3},{3,4},{4,5},{5,6},{6,7},{7,8},{8,9},{9,10},{10,1... | collective-permute-start | bytes 196616 | tf_op jit(solution)/shard_map/ppermute | solution.py:96
  79.5 6.4 %collective-permute-start.11 = (bf16[128,256]{0,1:T(8,128)(2,1)S(1)}, bf16[128,256]{0,1:T(8,128)(2,1)S(1)}, u32[]{:S(2)}, u32[]{:S(2)}) collective-permute-start(bf16[128,256]{0,1:T(8,128)(2,1)S(1)} %collective-permute-done.10), channel_id=1, source_target_pairs={{0,1},{1,2},{2,3},{3,4},{4,5},{5,6},{6,7},{7,8},{8,9},{9,10},{10,1... | collective-permute-start | bytes 196616 | tf_op jit(solution)/shard_map/ppermute | solution.py:96
  85.9 6.6 %collective-permute-start.12 = (bf16[128,256]{0,1:T(8,128)(2,1)S(1)}, bf16[128,256]{0,1:T(8,128)(2,1)S(1)}, u32[]{:S(2)}, u32[]{:S(2)}) collective-permute-start(bf16[128,256]{0,1:T(8,128)(2,1)S(1)} %collective-permute-done.11), channel_id=1, source_target_pairs={{0,1},{1,2},{2,3},{3,4},{4,5},{5,6},{6,7},{7,8},{8,9},{9,10},{10,1... | collective-permute-start | bytes 196616 | tf_op jit(solution)/shard_map/ppermute | solution.py:96
  92.5 6.4 %collective-permute-start.13 = (bf16[128,256]{0,1:T(8,128)(2,1)S(1)}, bf16[128,256]{0,1:T(8,128)(2,1)S(1)}, u32[]{:S(2)}, u32[]{:S(2)}) collective-permute-start(bf16[128,256]{0,1:T(8,128)(2,1)S(1)} %collective-permute-done.12), channel_id=1, source_target_pairs={{0,1},{1,2},{2,3},{3,4},{4,5},{5,6},{6,7},{7,8},{8,9},{9,10},{10,1... | collective-permute-start | bytes 196616 | tf_op jit(solution)/shard_map/ppermute | solution.py:96
  98.9 6.5 %collective-permute-start.14 = (bf16[128,256]{0,1:T(8,128)(2,1)S(1)}, bf16[128,256]{0,1:T(8,128)(2,1)S(1)}, u32[]{:S(2)}, u32[]{:S(2)}) collective-permute-start(bf16[128,256]{0,1:T(8,128)(2,1)S(1)} %collective-permute-done.13), channel_id=1, source_target_pairs={{0,1},{1,2},{2,3},{3,4},{4,5},{5,6},{6,7},{7,8},{8,9},{9,10},{10,1... | collective-permute-start | bytes 196616 | tf_op jit(solution)/shard_map/ppermute | solution.py:96
  105.7 7.8 %copy-start = (s32[2,1]{0,1:T(1,128)S(1)}, s32[2,1]{0,1:T(1,128)}, u32[]{:S(2)}) copy-start(s32[2,1]{0,1:T(1,128)} %param.11) | copy-start | bytes 28
Sparse Core Ops, SparseCore 0:
  74.9 38.6 all-gather.1
